TPU v7x, 32 devices: a whole 2x2x4 slice. The times are simulated.
32 devices in a mesh: rows: 8 (over z, y), cols: 4 (over x, core).
Axes of the slice: x: 2, y: 2, z: 4, core: 2. Of those that a mesh axis runs over, the one named last changes fastest.
Arguments:
- features: bfloat16 [64, 512, 512], P('rows', 'cols'), may hold values from -6 to 6
- dw_weight: float32 [49, 512], replicated, may hold values from -0.875 to 0.875
- norm_gain: float32 [512], replicated, may hold values from 0.1 to 1.9
- w_up: bfloat16 [512, 2048], replicated, may hold values from -0.25 to 0.25
- w_down: bfloat16 [2048, 512], replicated, may hold values from -0.125 to 0.125
- cotangent: bfloat16 [64, 512, 512], P('rows', 'cols'), may hold values from -6 to 6
Outputs:
- grad_input: bfloat16 [64, 512, 512], P('rows', 'cols')
- grad_dw: float32 [49, 512], replicated
- grad_gain: float32 [512], replicated
- grad_up: float32 [512, 2048], replicated
- grad_down: float32 [2048, 512], replicated
All inputs are finite; a program needn't handle non-finite values.
Results may differ from a plain program's by a relative error of at most 0.019.
Values may be sent and summed in bfloat16 or wider, within the bound.
No kernel may reach another device: no remote copies, remote signals or barrier semaphores. Data moves between devices by JAX's collectives and lax.ppermute only.
A program may use at most 128 MiB of HBM per device.

v0:
```python
import jax
import jax.numpy as jnp
from jax import lax
from jax.sharding import PartitionSpec as P

eps = 1e-06


def padded_2(block, sides, width):
    for axis, dim in sides:
        count = lax.axis_size(axis)
        forward = [(i, i + 1) for i in range(count - 1)]
        backward = [(target, source) for source, target in forward]
        low = lax.ppermute(
            lax.slice_in_dim(block, block.shape[dim] - width, None, axis=dim), axis, forward
        )
        high = lax.ppermute(lax.slice_in_dim(block, 0, width, axis=dim), axis, backward)
        block = jnp.concatenate([low, block, high], axis=dim)
    return block


def depthwise(padded, weight, rows, cols):
    total = jnp.zeros((rows, cols, padded.shape[2]), jnp.float32)
    for tap_i in range(7):
        for tap_j in range(7):
            total = (
                total
                + padded[tap_i : tap_i + rows, tap_j : tap_j + cols] * weight[7 * tap_i + tap_j]
            )
    return total


def pointwise(conv, gain, w_up, w_down, grad_out, keep):
    mean = jnp.mean(conv, axis=-1, keepdims=True)
    centred = conv - mean
    inv = lax.rsqrt(jnp.mean(centred * centred, axis=-1, keepdims=True) + eps)
    normed = centred * inv
    scaled = (normed * gain).astype(jnp.bfloat16)
    hidden = jnp.dot(scaled, w_up, preferred_element_type=jnp.float32)
    act = (0.5 * hidden * (1.0 + lax.erf(hidden * 0.7071067811865476))).astype(jnp.bfloat16)
    grad_kept = grad_out * keep.astype(jnp.bfloat16)
    grad_down = lax.dot_general(
        act, grad_kept, (((0,), (0,)), ((), ())), preferred_element_type=jnp.float32
    )
    grad_act = lax.dot_general(
        grad_out, w_down, (((1,), (1,)), ((), ())), preferred_element_type=jnp.float32
    )
    slope = (
        0.5 * (1.0 + lax.erf(hidden * 0.7071067811865476))
        + hidden * jnp.exp(-0.5 * hidden * hidden) * 0.3989422804014327
    )
    grad_hidden = (grad_act * slope).astype(jnp.bfloat16)
    hidden_kept = grad_hidden * keep.astype(jnp.bfloat16)
    grad_up = lax.dot_general(
        scaled, hidden_kept, (((0,), (0,)), ((), ())), preferred_element_type=jnp.float32
    )
    grad_scaled = lax.dot_general(
        grad_hidden, w_up, (((1,), (1,)), ((), ())), preferred_element_type=jnp.float32
    )
    grad_gain = jnp.sum(grad_scaled * normed * keep, axis=0)
    g_norm = grad_scaled * gain
    grad_conv = inv * (
        g_norm
        - jnp.mean(g_norm, axis=-1, keepdims=True)
        - normed * jnp.mean(g_norm * normed, axis=-1, keepdims=True)
    )
    return (grad_conv.astype(jnp.bfloat16), grad_up, grad_down, grad_gain)


def on_device(features, dw_weight, norm_gain, w_up, w_down, cotangent):
    rows, cols, chans = features.shape
    padded = padded_2(features, (("rows", 0), ("cols", 1)), 3).astype(jnp.float32)
    conv = depthwise(padded, dw_weight, rows, cols)
    keep = jnp.ones((rows * cols, 1), jnp.float32)
    grad_flat, grad_up, grad_down, grad_gain = pointwise(
        conv.reshape(rows * cols, chans),
        norm_gain,
        w_up,
        w_down,
        cotangent.reshape(rows * cols, chans),
        keep,
    )
    grad_conv = grad_flat.reshape(rows, cols, chans)
    grad_wide = padded_2(grad_conv, (("rows", 0), ("cols", 1)), 3)
    grad_f = grad_conv.astype(jnp.float32)
    taps = []
    for tap_i in range(7):
        for tap_j in range(7):
            taps.append(
                jnp.sum(padded[tap_i : tap_i + rows, tap_j : tap_j + cols] * grad_f, axis=(0, 1))
            )
    grad_dw = jnp.stack(taps)
    grad_pad = grad_wide.astype(jnp.float32)
    total = cotangent.astype(jnp.float32)
    for tap_i in range(7):
        for tap_j in range(7):
            total = (
                total
                + grad_pad[6 - tap_i : 6 - tap_i + rows, 6 - tap_j : 6 - tap_j + cols]
                * dw_weight[7 * tap_i + tap_j]
            )
    grad_input = total.astype(jnp.bfloat16)
    grad_up, grad_down, grad_dw, grad_gain = lax.psum(
        (grad_up, grad_down, grad_dw, grad_gain), ("rows", "cols")
    )
    return (grad_input, grad_dw, grad_gain, grad_up, grad_down)


def solution(mesh):
    return jax.shard_map(
        on_device,
        mesh=mesh,
        in_specs=(P("rows", "cols", None), P(), P(), P(), P(), P("rows", "cols", None)),
        out_specs=(P("rows", "cols", None), P(), P(), P(), P()),
        check_vma=False,
    )
```

profile of v0, /device:TPU:0, one launch (start us, length us, event | category | flops | bytes accessed | tf_op | source)
XLA Modules:
  0.0 353.4 jit_solution(14381172907683778319)
XLA Ops:
  7.2 1.4 fusion.113
  8.6 4.9 %collective-permute-start = (bf16[3,128,512]{2,1,0:T(8,128)(2,1)S(1)}, bf16[3,128,512]{2,1,0:T(8,128)(2,1)S(1)}, u32[]{:S(2)}, u32[]{:S(2)}) collective-permute-start(bf16[3,128,512]{2,1,0:T(8,128)(2,1)S(1)} %get-tuple-element.70), channel_id=1, source_target_pairs={{0,4},{4,8},{8,12},{12,16},{16,20},{20,24},{24,28},{1,5},{5,9},{9,... | collective-permute-start | bytes 1179656 | tf_op jit(solution)/shard_map/ppermute | solution.py:14
  13.5 1.3 collective-permute-start.1
  16.1 1.2 fusion.115
  17.5 12.8 %collective-permute-done = bf16[3,128,512]{2,1,0:T(8,128)(2,1)S(1)} collective-permute-done((bf16[3,128,512]{2,1,0:T(8,128)(2,1)S(1)}, bf16[3,128,512]{2,1,0:T(8,128)(2,1)S(1)}, u32[]{:S(2)}, u32[]{:S(2)}) %collective-permute-start) | collective-permute-done | bytes 393248 | tf_op jit(solution)/shard_map/ppermute | solution.py:14
  30.5 1.3 collective-permute-start.3
  31.8 3.0 collective-permute-start.2
  34.9 1.6 fusion.116
  36.5 2.5 maximum_convert_fusion
  39.4 54.0 %fusion.110 = (f32[8,128]{1,0:T(8,128)S(1)}, f32[8,128,512]{2,1,0:T(8,128)}) fusion(f32[512]{0:T(512)} %bitcast.48, f32[14,134,512]{2,1,0:T(8,128)} %maximum_convert_fusion, f32[512]{0:T(512)} %bitcast.47, f32[512]{0:T(512)S(1)} %bitcast.183, f32[512]{0:T(512)S(1)} %bitcast.185, f32[512]{0:T(512)S(1)} %bitcast.187, f32[512]{0:T(512)S(1)} %bitcast.189, ...), kind=kLoop, calls=%fused_computation.231 | loop fusion | flops 51379200 | bytes 104962048 | tf_op jit(solution)/shard_map/reduce_sum | solution.py:34
  93.4 2.1 multiply_reduce_fusion.2
  96.0 2.3 fusion.117
  98.4 5.0 %fusion.5 = bf16[1024,2048]{1,0:T(8,128)(2,1)S(1)} fusion(f32[1024,2048]{1,0:T(8,128)S(1)} %fusion.117, bf16[1024,512]{1,0:T(8,128)(2,1)S(1)} %bitcast.179, bf16[2048,512]{1,0:T(8,128)(2,1)S(1)} %copy-done.48), kind=kOutput, calls=%fused_computation.55 | convolution fusion | flops 2168455168 | bytes 15728640 | tf_op jit(solution)/shard_map/dot_general | solution.py:45
  103.5 3.4 multiply_reduce_fusion
  107.1 6.6 %fusion.56 = (f32[512]{0:T(512)}, f32[512]{0:T(512)}, f32[512]{0:T(512)}, f32[512]{0:T(512)}, f32[512]{0:T(512)}, /*index=5*/f32[512]{0:T(512)}, f32[512]{0:T(51...) fusion(f32[14,134,512]{2,1,0:T(8,128)S(1)} %copy-done.1, ...), kind=kLoop, calls=%fused_computation.108 | loop fusion | flops 23583744 | bytes 43046912 | tf_op jit(solution)/shard_map/reduce_sum | solution.py:90
  114.7 4.0 %fusion.20 = (f32[512]{0:T(512)}, f32[512]{0:T(512)}, f32[512]{0:T(512)}, f32[512]{0:T(512)}, f32[512]{0:T(512)}, /*index=5*/f32[512]{0:T(512)}, f32[512]{0:T(51...) fusion(f32[14,134,512]{2,1,0:T(8,128)S(1)} %copy-done.1, ...), kind=kLoop, calls=%fused_computation.72 | loop fusion | flops 14149120 | bytes 28338176 | tf_op jit(solution)/shard_map/reduce_sum | solution.py:90
  118.7 5.3 %fusion.38 = (f32[512]{0:T(512)}, f32[512]{0:T(512)}, f32[512]{0:T(512)}, f32[512]{0:T(512)}, f32[512]{0:T(512)}, /*index=5*/f32[512]{0:T(512)}, f32[512]{0:T(51...) fusion(f32[14,134,512]{2,1,0:T(8,128)S(1)} %copy-done.1, ...), kind=kLoop, calls=%fused_computation.90 | loop fusion | flops 19389440 | bytes 38834176 | tf_op jit(solution)/shard_map/reduce_sum | solution.py:90
  124.0 6.1 %fusion.6 = f32[2048,512]{1,0:T(8,128)} fusion(bf16[1024,512]{1,0:T(8,128)(2,1)S(1)} %bitcast.180, f32[1024,2048]{1,0:T(8,128)} %copy-done.49), kind=kOutput, calls=%fused_computation.58 | convolution fusion | flops 2157969408 | bytes 13631488 | tf_op jit(solution)/shard_map/dot_general | solution.py:42
  130.1 1.3 collective-permute-start.5
  131.4 5.8 %collective-permute-start.4 = (bf16[3,128,512]{2,1,0:T(8,128)(2,1)}, bf16[3,128,512]{2,1,0:T(8,128)(2,1)}, u32[]{:S(2)}, u32[]{:S(2)}) collective-permute-start(bf16[3,128,512]{2,1,0:T(8,128)(2,1)} %bitcast.53), channel_id=1, source_target_pairs={{0,4},{4,8},{8,12},{12,16},{16,20},{20,24},{24,28},{1,5},{5,9},{9,... | collective-permute-start | bytes 1179656 | tf_op jit(solution)/shard_map/ppermute | solution.py:14
  137.2 9.4 %stack.199 = f32[49,512]{1,0:T(8,128)} concatenate(f32[1,512]{1,0:T(1,128)} %bitcast.315, f32[1,512]{1,0:T(1,128)} %bitcast.314, f32[1,512]{1,0:T(1,128)} %bitcast.313, f32[1,512]{1,0:T(1,128)} %bitcast.312, f32[1,512]{1,0:T(1,128)} %bitcast.311, f32[1,512]{1,0:T(1,128)} %bitcast.310, f32[1,512]{1,0:T(1,128)} %bitcast.309, f32[1,512]{1,0:T(1,128)} %bitcast.308, ...), dimensions={0} | concatenate | bytes 200704 | tf_op jit(solution)/shard_map/stack | solution.py:92
  146.5 6.9 %fusion.118 = f32[512,2048]{1,0:T(8,128)} fusion(bf16[1024,512]{1,0:T(8,128)(2,1)} %copy-done.4, bf16[1024,2048]{1,0:T(8,128)(2,1)} %copy-done.3), kind=kOutput, calls=%fused_computation.239 | convolution fusion | flops 2147483648 | bytes 9437184 | tf_op jit(solution)/shard_map/dot_general | solution.py:54
  153.6 1.4 pad_maximum_fusion.2
  155.1 1.3 collective-permute-start.7
  156.3 3.9 %collective-permute-start.6 = (bf16[14,3,512]{2,1,0:T(4,128)(2,1)}, bf16[14,3,512]{2,1,0:T(4,128)(2,1)}, u32[]{:S(2)}, u32[]{:S(2)}) collective-permute-start(bf16[14,3,512]{2,1,0:T(4,128)(2,1)} %get-tuple-element.63), channel_id=1, source_target_pairs={{0,1},{1,2},{2,3},{4,5},{5,6},{6,7},{8,9},{9,10},{10,11},{12,13},{... | collective-permute-start | bytes 129032 | tf_op jit(solution)/shard_map/ppermute | solution.py:14
  160.2 44.4 %psum.29 = f32[512]{0:T(512)} all-reduce(f32[512]{0:T(512)} %get-tuple-element.54), channel_id=1, replica_groups=mesh['rows'=8,'cols'=4] {'rows','cols'}, use_global_device_ids=true, to_apply=%region_55.0 | all-reduce | flops 512 | bytes 4096 | tf_op jit(solution)/shard_map/psum | solution.py:103
  204.6 3.6 %maximum_convert_fusion.1 = f32[14,134,512]{2,1,0:T(8,128)} fusion(bf16[14,3,512]{2,1,0:T(4,128)(2,1)} %collective-permute-done.7, bf16[3,128,512]{2,1,0:T(8,128)(2,1)S(1)} %collective-permute-done.5, bf16[8,128,512]{2,1,0:T(8,128)(2,1)S(1)} %bitcast.178, bf16[3,128,512]{2,1,0:T(8,128)(2,1)} %collective-permute-done.4, ...), kind=kLoop, calls=%fused_computation.217 | loop fusion | flops 9605120 | bytes 5763072 | tf_op jit(solution)/shard_map/convert_element_type | solution.py:93
  208.1 52.3 %fusion.58 = bf16[8,128,512]{2,1,0:T(8,128)(2,1)} fusion(f32[14,134,512]{2,1,0:T(8,128)} %maximum_convert_fusion.1, bf16[8,128,512]{2,1,0:T(8,128)(2,1)} %param.11, f32[512]{0:T(512)} %bitcast.48, f32[512]{0:T(512)} %bitcast.47, f32[512]{0:T(512)S(1)} %bitcast.184, f32[512]{0:T(512)S(1)} %bitcast.186, f32[512]{0:T(512)S(1)} %bitcast.188, f32[512]{0:T(512)} %bitcast.190, ...), kind=kLoop, calls=%fused_computation.111 | loop fusion | flops 52428800 | bytes 104957952 | tf_op jit(solution)/shard_map/convert_element_type | solution.py:102
  260.4 77.8 %all-reduce.3.cloned.1.call-done = (f32[49,512]{1,0:T(8,128)}, f32[512,2048]{1,0:T(8,128)}, f32[2048,512]{1,0:T(8,128)}) async-done(((f32[49,512]{1,0:T(8,128)}, f32[512,2048]{1,0:T(8,128)}, f32[2048,512]{1,0:T(8,128)}), (f32[49,512]{1,0:T(8,128)}, f32[512,2048]{1,0:T(8,128)}, f32[2048,512]{1,0:T(8,128)})) %all-reduce.3.cloned.1.call-update) | async-done | bytes 8488976 | tf_op jit(solution)/shard_map/psum | solution.py:103
  338.2 1.6 copy.16
  339.7 4.8 %copy.17 = f32[512,2048]{1,0:T(8,128)} copy(f32[512,2048]{1,0:T(8,128)} %get-tuple-element.128) | data formatting | bytes 8388608
  344.6 2.0 copy.18
  (119 shorter events, 3.4 us)
Async XLA Ops:
  7.2 88.8 %copy-start = (bf16[512,2048]{1,0:T(8,128)(2,1)S(1)}, bf16[512,2048]{1,0:T(8,128)(2,1)}, u32[]{:S(2)}) copy-start(bf16[512,2048]{1,0:T(8,128)(2,1)} %param.9) | copy-start | bytes 6291460
  7.2 23.1 %copy-start.6 = (bf16[8,128,512]{2,1,0:T(8,128)(2,1)S(1)}, bf16[8,128,512]{2,1,0:T(8,128)(2,1)}, u32[]{:S(2)}) copy-start(bf16[8,128,512]{2,1,0:T(8,128)(2,1)} %param.6) | copy-start | bytes 3145732
  7.2 331.0 %all-reduce.3.cloned.1.call-start = ((), (), s32[]{:S(2)}) async-start(), calls=%async_computation | async-start | bytes 17006592 | tf_op jit(solution)/shard_map/psum | solution.py:103
  8.6 21.7 %collective-permute-start = (bf16[3,128,512]{2,1,0:T(8,128)(2,1)S(1)}, bf16[3,128,512]{2,1,0:T(8,128)(2,1)S(1)}, u32[]{:S(2)}, u32[]{:S(2)}) collective-permute-start(bf16[3,128,512]{2,1,0:T(8,128)(2,1)S(1)} %get-tuple-element.70), channel_id=1, source_target_pairs={{0,4},{4,8},{8,12},{12,16},{16,20},{20,24},{24,28},{1,5},{5,9},{9,... | collective-permute-start | bytes 1179656 | tf_op jit(solution)/shard_map/ppermute | solution.py:14
  13.5 16.9 %collective-permute-start.1 = (bf16[3,128,512]{2,1,0:T(8,128)(2,1)S(1)}, bf16[3,128,512]{2,1,0:T(8,128)(2,1)S(1)}, u32[]{:S(2)}, u32[]{:S(2)}) collective-permute-start(bf16[3,128,512]{2,1,0:T(8,128)(2,1)S(1)} %get-tuple-element.69), channel_id=1, source_target_pairs={{4,0},{8,4},{12,8},{16,12},{20,16},{24,20},{28,24},{5,1},{9,5},{13... | collective-permute-start | bytes 1179656 | tf_op jit(solution)/shard_map/ppermute | solution.py:17
  16.0 23.1 %copy-start.8 = (f32[1,512]{1,0:T(1,128)}, f32[1,512]{1,0:T(1,128)S(1)}, u32[]{:S(2)}) copy-start(f32[1,512]{1,0:T(1,128)S(1)} %get-tuple-element.75) | copy-start | bytes 6148
  16.0 23.1 %copy-start.9 = (f32[1,512]{1,0:T(1,128)}, f32[1,512]{1,0:T(1,128)S(1)}, u32[]{:S(2)}) copy-start(f32[1,512]{1,0:T(1,128)S(1)} %get-tuple-element.76) | copy-start | bytes 6148
  16.0 23.1 %copy-start.10 = (f32[1,512]{1,0:T(1,128)}, f32[1,512]{1,0:T(1,128)S(1)}, u32[]{:S(2)}) copy-start(f32[1,512]{1,0:T(1,128)S(1)} %get-tuple-element.77) | copy-start | bytes 6148
  16.0 23.1 %copy-start.11 = (f32[1,512]{1,0:T(1,128)}, f32[1,512]{1,0:T(1,128)S(1)}, u32[]{:S(2)}) copy-start(f32[1,512]{1,0:T(1,128)S(1)} %get-tuple-element.78) | copy-start | bytes 6148
  16.0 23.1 %copy-start.12 = (f32[1,512]{1,0:T(1,128)}, f32[1,512]{1,0:T(1,128)S(1)}, u32[]{:S(2)}) copy-start(f32[1,512]{1,0:T(1,128)S(1)} %get-tuple-element.79) | copy-start | bytes 6148
  16.0 23.1 %copy-start.13 = (f32[1,512]{1,0:T(1,128)}, f32[1,512]{1,0:T(1,128)S(1)}, u32[]{:S(2)}) copy-start(f32[1,512]{1,0:T(1,128)S(1)} %get-tuple-element.80) | copy-start | bytes 6148
  16.0 23.1 %copy-start.14 = (f32[1,512]{1,0:T(1,128)}, f32[1,512]{1,0:T(1,128)S(1)}, u32[]{:S(2)}) copy-start(f32[1,512]{1,0:T(1,128)S(1)} %get-tuple-element.81) | copy-start | bytes 6148
  16.0 23.1 %copy-start.15 = (f32[1,512]{1,0:T(1,128)}, f32[1,512]{1,0:T(1,128)S(1)}, u32[]{:S(2)}) copy-start(f32[1,512]{1,0:T(1,128)S(1)} %get-tuple-element.82) | copy-start | bytes 6148
  16.0 23.1 %copy-start.16 = (f32[1,512]{1,0:T(1,128)}, f32[1,512]{1,0:T(1,128)S(1)}, u32[]{:S(2)}) copy-start(f32[1,512]{1,0:T(1,128)S(1)} %get-tuple-element.83) | copy-start | bytes 6148
  16.0 23.1 %copy-start.17 = (f32[1,512]{1,0:T(1,128)}, f32[1,512]{1,0:T(1,128)S(1)}, u32[]{:S(2)}) copy-start(f32[1,512]{1,0:T(1,128)S(1)} %get-tuple-element.84) | copy-start | bytes 6148
  16.1 23.1 %copy-start.18 = (f32[1,512]{1,0:T(1,128)}, f32[1,512]{1,0:T(1,128)S(1)}, u32[]{:S(2)}) copy-start(f32[1,512]{1,0:T(1,128)S(1)} %get-tuple-element.85) | copy-start | bytes 6148
  16.1 23.1 %copy-start.19 = (f32[1,512]{1,0:T(1,128)}, f32[1,512]{1,0:T(1,128)S(1)}, u32[]{:S(2)}) copy-start(f32[1,512]{1,0:T(1,128)S(1)} %get-tuple-element.86) | copy-start | bytes 6148
  16.1 23.1 %copy-start.20 = (f32[1,512]{1,0:T(1,128)}, f32[1,512]{1,0:T(1,128)S(1)}, u32[]{:S(2)}) copy-start(f32[1,512]{1,0:T(1,128)S(1)} %get-tuple-element.87) | copy-start | bytes 6148
  16.1 23.1 %copy-start.21 = (f32[1,512]{1,0:T(1,128)}, f32[1,512]{1,0:T(1,128)S(1)}, u32[]{:S(2)}) copy-start(f32[1,512]{1,0:T(1,128)S(1)} %get-tuple-element.88) | copy-start | bytes 6148
  16.1 23.1 %copy-start.22 = (f32[1,512]{1,0:T(1,128)}, f32[1,512]{1,0:T(1,128)S(1)}, u32[]{:S(2)}) copy-start(f32[1,512]{1,0:T(1,128)S(1)} %get-tuple-element.89) | copy-start | bytes 6148
  17.3 21.9 %copy-start.23 = (f32[1,512]{1,0:T(1,128)}, f32[1,512]{1,0:T(1,128)S(1)}, u32[]{:S(2)}) copy-start(f32[1,512]{1,0:T(1,128)S(1)} %get-tuple-element.90) | copy-start | bytes 6148
  17.3 21.9 %copy-start.24 = (f32[1,512]{1,0:T(1,128)}, f32[1,512]{1,0:T(1,128)S(1)}, u32[]{:S(2)}) copy-start(f32[1,512]{1,0:T(1,128)S(1)} %get-tuple-element.91) | copy-start | bytes 6148
  17.3 21.9 %copy-start.25 = (f32[1,512]{1,0:T(1,128)}, f32[1,512]{1,0:T(1,128)S(1)}, u32[]{:S(2)}) copy-start(f32[1,512]{1,0:T(1,128)S(1)} %get-tuple-element.92) | copy-start | bytes 6148
  17.3 21.9 %copy-start.26 = (f32[1,512]{1,0:T(1,128)}, f32[1,512]{1,0:T(1,128)S(1)}, u32[]{:S(2)}) copy-start(f32[1,512]{1,0:T(1,128)S(1)} %get-tuple-element.93) | copy-start | bytes 6148
  17.3 21.9 %copy-start.27 = (f32[1,512]{1,0:T(1,128)}, f32[1,512]{1,0:T(1,128)S(1)}, u32[]{:S(2)}) copy-start(f32[1,512]{1,0:T(1,128)S(1)} %get-tuple-element.94) | copy-start | bytes 6148
  17.3 21.9 %copy-start.28 = (f32[1,512]{1,0:T(1,128)}, f32[1,512]{1,0:T(1,128)S(1)}, u32[]{:S(2)}) copy-start(f32[1,512]{1,0:T(1,128)S(1)} %get-tuple-element.95) | copy-start | bytes 6148
  30.5 6.0 %collective-permute-start.3 = (bf16[14,3,512]{2,1,0:T(4,128)(2,1)S(1)}, bf16[14,3,512]{2,1,0:T(4,128)(2,1)S(1)}, u32[]{:S(2)}, u32[]{:S(2)}) collective-permute-start(bf16[14,3,512]{2,1,0:T(4,128)(2,1)S(1)} %get-tuple-element.66), channel_id=1, source_target_pairs={{1,0},{2,1},{3,2},{5,4},{6,5},{7,6},{9,8},{10,9},{11,10},{13,12},{... | collective-permute-start | bytes 129032 | tf_op jit(solution)/shard_map/ppermute | solution.py:17
  31.8 4.7 %collective-permute-start.2 = (bf16[14,3,512]{2,1,0:T(4,128)(2,1)S(1)}, bf16[14,3,512]{2,1,0:T(4,128)(2,1)S(1)}, u32[]{:S(2)}, u32[]{:S(2)}) collective-permute-start(bf16[14,3,512]{2,1,0:T(4,128)(2,1)S(1)} %get-tuple-element.65), channel_id=1, source_target_pairs={{0,1},{1,2},{2,3},{4,5},{5,6},{6,7},{8,9},{9,10},{10,11},{12,13},{... | collective-permute-start | bytes 129032 | tf_op jit(solution)/shard_map/ppermute | solution.py:14
  130.1 23.3 %collective-permute-start.5 = (bf16[3,128,512]{2,1,0:T(8,128)(2,1)}, bf16[3,128,512]{2,1,0:T(8,128)(2,1)S(1)}, u32[]{:S(2)}, u32[]{:S(2)}) collective-permute-start(bf16[3,128,512]{2,1,0:T(8,128)(2,1)} %bitcast.55), channel_id=1, source_target_pairs={{4,0},{8,4},{12,8},{16,12},{20,16},{24,20},{28,24},{5,1},{9,5},{13... | collective-permute-start | bytes 1179656 | tf_op jit(solution)/shard_map/ppermute | solution.py:17
  131.4 22.2 %collective-permute-start.4 = (bf16[3,128,512]{2,1,0:T(8,128)(2,1)}, bf16[3,128,512]{2,1,0:T(8,128)(2,1)}, u32[]{:S(2)}, u32[]{:S(2)}) collective-permute-start(bf16[3,128,512]{2,1,0:T(8,128)(2,1)} %bitcast.53), channel_id=1, source_target_pairs={{0,4},{4,8},{8,12},{12,16},{16,20},{20,24},{24,28},{1,5},{5,9},{9,... | collective-permute-start | bytes 1179656 | tf_op jit(solution)/shard_map/ppermute | solution.py:14
  155.1 49.5 %collective-permute-start.7 = (bf16[14,3,512]{2,1,0:T(4,128)(2,1)}, bf16[14,3,512]{2,1,0:T(4,128)(2,1)}, u32[]{:S(2)}, u32[]{:S(2)}) collective-permute-start(bf16[14,3,512]{2,1,0:T(4,128)(2,1)} %get-tuple-element.64), channel_id=1, source_target_pairs={{1,0},{2,1},{3,2},{5,4},{6,5},{7,6},{9,8},{10,9},{11,10},{13,12},{... | collective-permute-start | bytes 129032 | tf_op jit(solution)/shard_map/ppermute | solution.py:17
  156.3 48.2 %collective-permute-start.6 = (bf16[14,3,512]{2,1,0:T(4,128)(2,1)}, bf16[14,3,512]{2,1,0:T(4,128)(2,1)}, u32[]{:S(2)}, u32[]{:S(2)}) collective-permute-start(bf16[14,3,512]{2,1,0:T(4,128)(2,1)} %get-tuple-element.63), channel_id=1, source_target_pairs={{0,1},{1,2},{2,3},{4,5},{5,6},{6,7},{8,9},{9,10},{10,11},{12,13},{... | collective-permute-start | bytes 129032 | tf_op jit(solution)/shard_map/ppermute | solution.py:14
  (27 other events, 327.8 us)
Sparse Core Ops, SparseCore 0:
  153.6 184.5 all-reduce.2
where the time goes:
time: 354 us; the launch traced here: 353 us
  other arithmetic  132 us (37%)
  waiting for transfers between devices  90.8 us (26%)
  blocking collectives  44.4 us (13%)
  local copies, waits for them, and re-layouts  24.7 us (7%)
  matrix products  23.8 us (7%)
  starting transfers between devices  22.8 us (6%)
  between operations  14.9 us (4%)
    psum x1, waiting for transfers between devices, on_device(): lax.psum((grad_up, grad_down, grad_dw, grad_gain), ('rows', 'cols'))  77.8 us
    reduce_sum x1, other arithmetic, pointwise(): mean = jnp.mean(conv, axis=-1, keepdims=True)  54 us
    convert_element_type x1, other arithmetic, on_device(): grad_input = total.astype(jnp.bfloat16)  52.3 us
    psum x1, blocking collectives, on_device(): lax.psum((grad_up, grad_down, grad_dw, grad_gain), ('rows', 'cols'))  44.4 us
    ppermute x4, starting transfers between devices, padded_2(): lax.ppermute(lax.slice_in_dim(block, block.shape[dim] - width, None, axis...  17.6 us
    reduce_sum x3, other arithmetic, on_device(): jnp.sum(padded[tap_i:tap_i + rows, tap_j:tap_j + cols] * grad_f, axis=(0,...  15.9 us
    ppermute x4, waiting for transfers between devices, padded_2(): lax.ppermute(lax.slice_in_dim(block, block.shape[dim] - width, None, axis...  13 us
    another operation x1, local copies, waits for them, and re-layouts, on_device(): grad_dw = jnp.stack(taps)  9.36 us
  transfers between devices with their start and end apart: 9, of which 3 were waited for; matrix products, arithmetic and copies ran while one was open for 22% of the time, Pallas kernels for 0%

commit v1 on v0

v1 whole, which is shorter than its diff:
```python
import functools
import jax, jax.numpy as jnp
from jax import lax
from jax.sharding import PartitionSpec as P
from jax.experimental import pallas as pl
from jax.experimental.pallas import tpu as pltpu
bf16, f32 = jnp.bfloat16, jnp.float32
VM = pl.BlockSpec(memory_space=pltpu.VMEM)
PADC = 8

def fill(xs, x_ref, top, bot, lft, rgt, ctop, cbot, r, c, nb):
    def put(row0, nrow, col0, ref):
        ncol = ref.shape[1]
        for b in range(nb):
            xs[row0:row0 + nrow, b, col0:col0 + ncol, :] = ref[:, :, b * 128:(b + 1) * 128].astype(f32)
    put(3, r, PADC, x_ref)
    put(0, 3, PADC, top)
    put(r + 3, 3, PADC, bot)
    put(3, r, PADC - 3, lft)
    put(3, r, PADC + c, rgt)
    for b in range(nb):
        s = slice(b * 128, (b + 1) * 128)
        xs[0:3, b, PADC - 3:PADC, :] = ctop[:, 0:3, s].astype(f32)
        xs[0:3, b, PADC + c:PADC + c + 3, :] = ctop[:, 3:6, s].astype(f32)
        xs[r + 3:r + 6, b, PADC - 3:PADC, :] = cbot[:, 0:3, s].astype(f32)
        xs[r + 3:r + 6, b, PADC + c:PADC + c + 3, :] = cbot[:, 3:6, s].astype(f32)

def conv_into(out, xs, w_ref, r, c, nb, flip, base=None, unroll=2):
    def body(t, _):
        b = t // (c // (8 * unroll))
        k = t % (c // (8 * unroll))
        c0 = pl.multiple_of(k * (8 * unroll), 8 * unroll)
        lane = pl.multiple_of(b * 128, 128)
        acc = [[None] * unroll for _ in range(r)]
        if base is not None:
            for o in range(r):
                blk = base[o, pl.ds(c0, 8 * unroll), pl.ds(lane, 128)].astype(f32)
                for u in range(unroll):
                    acc[o][u] = blk[8 * u:8 * u + 8]
        for j in range(7):
            ws = []
            for i in range(7):
                tap = 7 * i + j
                if flip: tap = 48 - tap
                ws.append(jnp.broadcast_to(w_ref[tap:tap + 1, pl.ds(lane, 128)], (8, 128)))
            for q in range(r + 6):
                for u in range(unroll):
                    v = xs[q, b, pl.ds(c0 + 8 * u + PADC - 3 + j, 8), :]
                    for i in range(7):
                        o = q - i
                        if 0 <= o < r:
                            p = v * ws[i]
                            acc[o][u] = p if acc[o][u] is None else acc[o][u] + p
        for o in range(r):
            blk = jnp.concatenate(acc[o], axis=0)
            out[o, pl.ds(c0, 8 * unroll), pl.ds(lane, 128)] = blk.astype(out.dtype)
        return 0
    lax.fori_loop(0, nb * (c // (8 * unroll)), body, 0)

def fwd_kernel(x_ref, top, bot, lft, rgt, ctop, cbot, w_ref, gain, scaled, scaled_t, normed, inv_ref, xs):
    r, c, ch = x_ref.shape
    nb = ch // 128
    fill(xs, x_ref, top, bot, lft, rgt, ctop, cbot, r, c, nb)
    conv_into(normed, xs, w_ref, r, c, nb, False)
    g = gain[...]
    def ln(t, _):
        o = t
        x = normed[o]
        mean = jnp.mean(x, axis=-1, keepdims=True)
        cen = x - mean
        inv = lax.rsqrt(jnp.mean(cen * cen, axis=-1, keepdims=True) + 1e-6)
        nrm = cen * inv
        normed[o] = nrm
        inv_ref[o] = jnp.broadcast_to(inv, (c, 128))
        sc = (nrm * g).astype(bf16)
        scaled[o] = sc
        scaled_t[:, pl.ds(pl.multiple_of(o * c, c), c)] = sc.T
        return 0
    lax.fori_loop(0, r, ln, 0)

def forward(x, top, bot, lft, rgt, ctop, cbot, w, gain):
    r, c, ch = x.shape
    S = jax.ShapeDtypeStruct
    return pl.pallas_call(
        fwd_kernel,
        out_shape=(S((r, c, ch), bf16), S((ch, r * c), bf16), S((r, c, ch), f32), S((r, c, 128), f32)),
        in_specs=[VM] * 9, out_specs=(VM,) * 4,
        scratch_shapes=[pltpu.VMEM((r + 6, ch // 128, c + 16, 128), f32)],
        compiler_params=pltpu.CompilerParams(vmem_limit_bytes=48 << 20),
        name="conv_norm",
    )(x, top, bot, lft, rgt, ctop, cbot, w, gain)

NT = (((1,), (1,)), ((), ()))
def mlp_kernel(scaled, scaled_t, cot, cot_t, w_up, w_down, gd, gu, gh_out, *, fc):
    ff = w_up.shape[1]
    def body(k, _):
        f0 = pl.multiple_of(k * fc, fc)
        h = jnp.dot(scaled[...], w_up[:, pl.ds(f0, fc)], preferred_element_type=f32)
        ga = lax.dot_general(cot[...], w_down[pl.ds(f0, fc), :], NT, preferred_element_type=f32)
        phi = 0.5 + 0.5 * lax.erf(h * 0.7071067811865476)
        act = (h * phi).astype(bf16)
        slope = phi + h * (jnp.exp(-0.5 * h * h) * 0.3989422804014327)
        gh = (ga * slope).astype(bf16)
        gh_out[:, pl.ds(f0, fc)] = gh
        gd[:, pl.ds(f0, fc)] = jnp.dot(cot_t[...], act, preferred_element_type=f32).astype(gd.dtype)
        gu[:, pl.ds(f0, fc)] = jnp.dot(scaled_t[...], gh, preferred_element_type=f32).astype(gu.dtype)
        return 0
    lax.fori_loop(0, ff // fc, body, 0)

def mlp(scaled, scaled_t, cot, cot_t, w_up, w_down, fc=256):
    n, ch = scaled.shape
    ff = w_up.shape[1]
    S = jax.ShapeDtypeStruct
    return pl.pallas_call(
        functools.partial(mlp_kernel, fc=fc),
        out_shape=(S((ch, ff), bf16), S((ch, ff), bf16), S((n, ff), bf16)),
        in_specs=[VM] * 6, out_specs=(VM,) * 3,
        compiler_params=pltpu.CompilerParams(vmem_limit_bytes=48 << 20),
        name="mlp",
    )(scaled, scaled_t, cot, cot_t, w_up, w_down)

def back_kernel(gh, w_up, normed, inv_ref, gain, gc, gg):
    n, ch = normed.shape
    rb = 256
    g = gain[...]
    def body(k, tot):
        r0 = pl.multiple_of(k * rb, rb)
        gs = lax.dot_general(gh[pl.ds(r0, rb), :], w_up[...], NT, preferred_element_type=f32)
        nrm = normed[pl.ds(r0, rb), :]
        inv = inv_ref[pl.ds(r0, rb), 0:1]
        gn = gs * nrm
        tot = tot + jnp.sum(gn.reshape(rb // 8, 8, ch), axis=0)
        m1 = jnp.mean(gs * g, axis=-1, keepdims=True)
        m2 = jnp.mean(gn * g, axis=-1, keepdims=True)
        gc[pl.ds(r0, rb), :] = (inv * (gs * g - m1 - nrm * m2)).astype(bf16)
        return tot
    tot = lax.fori_loop(0, n // rb, body, jnp.zeros((8, ch), f32))
    gg[...] = jnp.sum(tot, axis=0, keepdims=True)

def back(gh, w_up, normed, inv, gain):
    n, ch = normed.shape
    S = jax.ShapeDtypeStruct
    return pl.pallas_call(
        back_kernel, out_shape=(S((n, ch), bf16), S((1, ch), f32)),
        in_specs=[VM] * 5, out_specs=(VM,) * 2,
        compiler_params=pltpu.CompilerParams(vmem_limit_bytes=48 << 20), name="norm_back",
    )(gh, w_up, normed, inv, gain)

def taps_kernel(x_ref, top, bot, lft, rgt, ctop, cbot, gc, gg, dw, xs, gf):
    r, c, ch = x_ref.shape
    nb = ch // 128
    fill(xs, x_ref, top, bot, lft, rgt, ctop, cbot, r, c, nb)
    dw[...] = jnp.zeros(dw.shape, dw.dtype)
    for b in range(nb):
        gf[:, b] = gc[:, :, b * 128:(b + 1) * 128].astype(f32)
    def body(b, _):
        lane = pl.multiple_of(b * 128, 128)
        for j in range(7):
            def inner(k, acc):
                c0 = pl.multiple_of(k * 8, 8)
                gs = [gf[o, b, pl.ds(c0, 8), :] for o in range(r)]
                acc = list(acc)
                for q in range(r + 6):
                    v = xs[q, b, pl.ds(c0 + PADC - 3 + j, 8), :]
                    for i in range(7):
                        o = q - i
                        if 0 <= o < r:
                            acc[i] = acc[i] + v * gs[o]
                return tuple(acc)
            acc = lax.fori_loop(0, c // 8, inner, tuple(jnp.zeros((8, 128), f32) for _ in range(7)), unroll=4)
            for i in range(7):
                tap = 7 * i + j
                dw[tap:tap + 1, pl.ds(lane, 128)] = jnp.sum(acc[i], axis=0, keepdims=True)
        return 0
    lax.fori_loop(0, nb, body, 0)
    dw[49:50, :] = gg[...]

def taps(x, top, bot, lft, rgt, ctop, cbot, gc, gg):
    r, c, ch = x.shape
    S = jax.ShapeDtypeStruct
    return pl.pallas_call(
        taps_kernel, out_shape=S((56, ch), f32), in_specs=[VM] * 9, out_specs=VM,
        scratch_shapes=[pltpu.VMEM((r + 6, ch // 128, c + 16, 128), f32), pltpu.VMEM((r, ch // 128, c, 128), f32)],
        compiler_params=pltpu.CompilerParams(vmem_limit_bytes=48 << 20), name="tap_sums",
    )(x, top, bot, lft, rgt, ctop, cbot, gc, gg)

def spread_kernel(x_ref, top, bot, lft, rgt, ctop, cbot, w_ref, cot, out, xs):
    r, c, ch = x_ref.shape
    nb = ch // 128
    fill(xs, x_ref, top, bot, lft, rgt, ctop, cbot, r, c, nb)
    conv_into(out, xs, w_ref, r, c, nb, True, base=cot)

def spread(x, top, bot, lft, rgt, ctop, cbot, w, cot):
    r, c, ch = x.shape
    return pl.pallas_call(
        spread_kernel, out_shape=jax.ShapeDtypeStruct((r, c, ch), bf16), in_specs=[VM] * 9, out_specs=VM,
        scratch_shapes=[pltpu.VMEM((r + 6, ch // 128, c + 16, 128), f32)],
        compiler_params=pltpu.CompilerParams(vmem_limit_bytes=48 << 20), name="spread",
    )(x, top, bot, lft, rgt, ctop, cbot, w, cot)


def ring_shift(block, axis, step):
    count = lax.axis_size(axis)
    pairs = [(i, i + step) for i in range(count) if 0 <= i + step < count]
    return lax.ppermute(block, axis, pairs)


def halo(block):
    r, c = block.shape[:2]
    lft = ring_shift(block[:, c - 3:], "cols", 1)
    rgt = ring_shift(block[:, :3], "cols", -1)
    top = ring_shift(block[r - 3:], "rows", 1)
    bot = ring_shift(block[:3], "rows", -1)
    side = jnp.concatenate([lft, rgt], axis=1)
    ctop = ring_shift(side[r - 3:], "rows", 1)
    cbot = ring_shift(side[:3], "rows", -1)
    return block, top, bot, lft, rgt, ctop, cbot


def bits_of(axis):
    count = lax.axis_size(axis)
    assert count & (count - 1) == 0
    return [(axis, 1 << k) for k in range(count.bit_length() - 1)]


def swap(block, axis, bit):
    return lax.ppermute(block, axis, [(i, i ^ bit) for i in range(lax.axis_size(axis))])


def side_of(axis, bit):
    return (lax.axis_index(axis) // bit) % 2


def total_sum(block, order):
    for axis, bit in order:
        half = block.shape[0] // 2
        side = side_of(axis, bit)
        keep = lax.dynamic_slice_in_dim(block, side * half, half, 0)
        send = lax.dynamic_slice_in_dim(block, (1 - side) * half, half, 0)
        got = swap(send, axis, bit)
        block = (keep.astype(f32) + got.astype(f32)).astype(bf16)
    for axis, bit in reversed(order):
        side = side_of(axis, bit)
        got = swap(block, axis, bit)
        low = jnp.where(side == 0, block, got)
        high = jnp.where(side == 0, got, block)
        block = jnp.concatenate([low, high], axis=0)
    return block


def small_sum(block, order):
    for axis, bit in order:
        mine = block.astype(bf16)
        block = mine.astype(f32) + swap(mine, axis, bit).astype(f32)
    return block


def on_device(features, dw_weight, norm_gain, w_up, w_down, cotangent):
    r, c, ch = features.shape
    n = r * c
    gain = norm_gain.reshape(1, ch)
    cot = cotangent.reshape(n, ch)
    padded = halo(features)
    scaled, scaled_t, normed, inv = forward(*padded, dw_weight, gain)
    gd_t, gu, gh = mlp(scaled.reshape(n, ch), scaled_t, cot, cot.T, w_up, w_down)
    cols, rows = bits_of("cols"), bits_of("rows")
    gd_t = total_sum(gd_t, cols + rows)
    gu = total_sum(gu, cols[:1] + rows + cols[1:])
    gc, gg = back(gh, w_up, normed.reshape(n, ch), inv.reshape(n, 128), gain)
    gc = gc.reshape(r, c, ch)
    wide = halo(gc)
    small = taps(*padded, gc, gg)
    small = small_sum(small, cols + rows)
    grad_input = spread(*wide, dw_weight, cotangent)
    return (grad_input, small[:49], small[49], gu.astype(f32), gd_t.T.astype(f32))


def solution(mesh):
    tile, whole = P("rows", "cols", None), P()
    return jax.shard_map(
        on_device,
        mesh=mesh,
        in_specs=(tile, whole, whole, whole, whole, tile),
        out_specs=(tile, whole, whole, whole, whole),
        check_vma=False,
    )
```

time: 354 us -> 258 us (0.73)
  other arithmetic: 132 us -> 10.2 us
  Pallas kernels: 0 us -> 60.8 us
  blocking collectives: 44.4 us -> 0 us
  waiting for transfers between devices: 90.8 us -> 124 us
  starting transfers between devices: 22.8 us -> 48.2 us
  matrix products: 23.8 us -> 0 us
  between operations: 14.9 us -> 1.49 us
  local copies, waits for them, and re-layouts: 24.7 us -> 12.5 us
    ppermute x8 -> x37, waiting for transfers between devices: 13 us -> 124 us  [the longest x25 115 us: swap(): lax.ppermute(block, axis, [(i, i ^ bit) for i in range(lax.axis_size(axis...]
    psum x1 -> x0, waiting for transfers between devices: 77.8 us -> none  [on_device(): lax.psum((grad_up, grad_down, grad_dw, grad_gain), ('rows', 'cols'))]
    reduce_sum x5 -> x0, other arithmetic: 72 us -> none  [the longest x1 54 us: pointwise(): mean = jnp.mean(conv, axis=-1, keepdims=True)]
    pallas_call x0 -> x5, Pallas kernels: none -> 60.8 us  [the longest x1 17.9 us: mlp(): pl.pallas_call(functools.partial(mlp_kernel, fc=fc), out_shape=(S((ch, ff...]
    convert_element_type x4 -> x17, other arithmetic: 58.7 us -> 6.47 us  [the longest x1 2.56 us: on_device(): gu.astype(f32)]
    psum x1 -> x0, blocking collectives: 44.4 us -> none  [on_device(): lax.psum((grad_up, grad_down, grad_dw, grad_gain), ('rows', 'cols'))]
    ppermute x8 -> x37, starting transfers between devices: 22.7 us -> 48.2 us  [the longest x12 31.6 us: ring_shift(): return lax.ppermute(block, axis, pairs)]
    dot_general x5 -> x0, matrix products: 23.8 us -> none  [the longest x1 6.9 us: pointwise(): lax.dot_general(scaled, hidden_kept, (((0,), (0,)), ((), ())), preferred_...]
  transfers between devices with their start and end apart: 9 -> 37, of which waited for: 3 -> 25; matrix products, arithmetic and copies ran while one was open for 22% -> 6% of each run, Pallas kernels for 0% -> 8%
where the time goes in v1:
time: 258 us; the launch traced here: 257 us
  waiting for transfers between devices  124 us (48%)
  Pallas kernels  60.8 us (24%)
  starting transfers between devices  48.2 us (19%)
  local copies, waits for them, and re-layouts  12.5 us (5%)
  other arithmetic  10.2 us (4%)
    ppermute x25, waiting for transfers between devices, swap(): lax.ppermute(block, axis, [(i, i ^ bit) for i in range(lax.axis_size(axis...  115 us
    ppermute x12, starting transfers between devices, ring_shift(): return lax.ppermute(block, axis, pairs)  31.6 us
    pallas_call x1, Pallas kernels, mlp(): pl.pallas_call(functools.partial(mlp_kernel, fc=fc), out_shape=(S((ch, ff...  17.9 us
    ppermute x25, starting transfers between devices, swap(): lax.ppermute(block, axis, [(i, i ^ bit) for i in range(lax.axis_size(axis...  16.6 us
    pallas_call x1, Pallas kernels, forward(): pl.pallas_call(fwd_kernel, out_shape=(S((r, c, ch), bf16), S((ch, r * c),...  15.4 us
    pallas_call x1, Pallas kernels, spread(): pl.pallas_call(spread_kernel, out_shape=jax.ShapeDtypeStruct((r, c, ch),...  12.5 us
    ppermute x12, waiting for transfers between devices, ring_shift(): return lax.ppermute(block, axis, pairs)  9.52 us
    pallas_call x1, Pallas kernels, taps(): pl.pallas_call(taps_kernel, out_shape=S((56, ch), f32), in_specs=[VM] * 9...  9.37 us
  transfers between devices with their start and end apart: 37, of which 25 were waited for; matrix products, arithmetic and copies ran while one was open for 6% of the time, Pallas kernels for 8%

profile of v1, /device:TPU:0, one launch (start us, length us, event | category | flops | bytes accessed | tf_op | source)
XLA Modules:
  0.0 257.5 jit_solution(10346830520634909648)
XLA Ops:
  2.9 4.9 %collective-permute-start = (bf16[3,128,512]{2,1,0:T(8,128)(2,1)}, bf16[3,128,512]{2,1,0:T(8,128)(2,1)S(1)}, u32[]{:S(2)}, u32[]{:S(2)}) collective-permute-start(bf16[3,128,512]{2,1,0:T(8,128)(2,1)} %get-tuple-element.43), channel_id=1, source_target_pairs={{0,4},{4,8},{8,12},{12,16},{16,20},{20,24},{24,28},{1,5},{5,9},{9,... | collective-permute-start | bytes 1179656 | tf_op jit(solution)/shard_map/ppermute | solution.py:205
  12.8 3.3 %collective-permute-done.3.rgt = bf16[8,3,512]{2,1,0:T(4,128)(2,1)S(1)} collective-permute-done((bf16[8,3,512]{2,1,0:T(4,128)(2,1)S(1)}, bf16[8,3,512]{2,1,0:T(4,128)(2,1)S(1)}, u32[]{:S(2)}, u32[]{:S(2)}) %collective-permute-start.3) | collective-permute-done | bytes 24608 | tf_op jit(solution)/shard_map/ppermute | solution.py:205
  16.8 5.1 %collective-permute-start.4 = (bf16[3,6,512]{2,1,0:T(8,128)(2,1)}, bf16[3,6,512]{2,1,0:T(8,128)(2,1)}, u32[]{:S(2)}, u32[]{:S(2)}) collective-permute-start(bf16[3,6,512]{2,1,0:T(8,128)(2,1)} %get-tuple-element.59), channel_id=1, source_target_pairs={{0,4},{4,8},{8,12},{12,16},{16,20},{20,24},{24,28},{1,5},{5,9},{9,... | collective-permute-start | bytes 55304 | tf_op jit(solution)/shard_map/ppermute | solution.py:205
  25.3 2.7 %collective-permute-done.5.cbot = bf16[3,6,512]{2,1,0:T(8,128)(2,1)} collective-permute-done((bf16[3,6,512]{2,1,0:T(8,128)(2,1)}, bf16[3,6,512]{2,1,0:T(8,128)(2,1)}, u32[]{:S(2)}, u32[]{:S(2)}) %collective-permute-start.5) | collective-permute-done | bytes 18464 | tf_op jit(solution)/shard_map/ppermute | solution.py:205
  30.4 15.4 %conv_norm.1 = (bf16[8,128,512]{2,1,0:T(8,128)(2,1)S(1)}, bf16[512,1024]{1,0:T(8,128)(2,1)S(1)}, f32[8,128,512]{2,1,0:T(8,128)}, f32[8,128,128]{2,1,0:T(8,128)S(1)}) custom-call(bf16[8,128,512]{2,1,0:T(8,128)(2,1)S(1)} %copy-done.2, bf16[3,128,512]{2,1,0:T(8,128)(2,1)S(1)} %collective-permute-done.top, bf16[3,128,512]{2,1,0:T(8,128)(2,1)} %collective-permute-done.1.bot, ...), custom_call_target="tpu_custom_call" | custom-call | tf_op jit(solution)/shard_map/conv_norm/pallas_call | solution.py:84
  45.8 17.9 %mlp.1 = (bf16[512,2048]{1,0:T(8,128)(2,1)}, bf16[512,2048]{1,0:T(8,128)(2,1)}, bf16[1024,2048]{1,0:T(8,128)(2,1)}) custom-call(bf16[1024,512]{1,0:T(8,128)(2,1)S(1)} %bitcast.20, bf16[512,1024]{1,0:T(8,128)(2,1)S(1)} %get-tuple-element.15.scaled_t, bf16[1024,512]{1,0:T(8,128)(2,1)S(1)} %bitcast.14, bf16[512,1024]{1,0:T(8,128)(2,1)S(1)} %bitcast.18, ...), custom_call_target="tpu_custom_call" | custom-call | tf_op jit(solution)/shard_map/mlp/pallas_call | solution.py:114
  63.6 5.7 %norm_back.1 = (bf16[1024,512]{1,0:T(8,128)(2,1)S(1)}, f32[1,512]{1,0:T(1,128)S(1)}) custom-call(bf16[1024,2048]{1,0:T(8,128)(2,1)} %get-tuple-element.16.gh, bf16[512,2048]{1,0:T(8,128)(2,1)S(1)} %copy-done.1, f32[1024,512]{1,0:T(8,128)S(1)} %bitcast.19, f32[1024,128]{1,0:T(8,128)S(1)} %bitcast.21, f32[1,512]{1,0:T(1,128)S(1)} %bitcast.23), custom_call_target="tpu_custom_call" | custom-call | tf_op jit(solution)/shard_map/norm_back/pallas_call | solution.py:143
  69.4 4.7 %collective-permute-start.6 = (bf16[3,128,512]{2,1,0:T(8,128)(2,1)S(1)}, bf16[3,128,512]{2,1,0:T(8,128)(2,1)S(1)}, u32[]{:S(2)}, u32[]{:S(2)}) collective-permute-start(bf16[3,128,512]{2,1,0:T(8,128)(2,1)S(1)} %bitcast.25), channel_id=1, source_target_pairs={{0,4},{4,8},{8,12},{12,16},{16,20},{20,24},{24,28},{1,5},{5,9},{9,... | collective-permute-start | bytes 1179656 | tf_op jit(solution)/shard_map/ppermute | solution.py:205
  75.5 3.3 %collective-permute-start.8 = (bf16[8,3,512]{2,1,0:T(4,128)(2,1)S(1)}, bf16[8,3,512]{2,1,0:T(4,128)(2,1)S(1)}, u32[]{:S(2)}, u32[]{:S(2)}) collective-permute-start(bf16[8,3,512]{2,1,0:T(4,128)(2,1)S(1)} %get-tuple-element.37), channel_id=1, source_target_pairs={{0,1},{1,2},{2,3},{4,5},{5,6},{6,7},{8,9},{9,10},{10,11},{12,13},{... | collective-permute-start | bytes 73736 | tf_op jit(solution)/shard_map/ppermute | solution.py:205
  78.8 9.4 %tap_sums.1 = f32[56,512]{1,0:T(8,128)S(1)} custom-call(bf16[8,128,512]{2,1,0:T(8,128)(2,1)S(1)} %copy-done.2, bf16[3,128,512]{2,1,0:T(8,128)(2,1)S(1)} %collective-permute-done.top, bf16[3,128,512]{2,1,0:T(8,128)(2,1)} %collective-permute-done.1.bot, bf16[8,3,512]{2,1,0:T(4,128)(2,1)S(1)} %copy-done.6, bf16[8,3,512]{2,1,0:T(4,128)(2,1)S(1)} %copy-done.8, ...), custom_call_target="tpu_custom_call" | custom-call | tf_op jit(solution)/shard_map/tap_sums/pallas_call | solution.py:181
  90.9 3.9 %collective-permute-done.13 = bf16[56,512]{1,0:T(8,128)(2,1)S(1)} collective-permute-done((bf16[56,512]{1,0:T(8,128)(2,1)S(1)}, bf16[56,512]{1,0:T(8,128)(2,1)S(1)}, u32[]{:S(2)}, u32[]{:S(2)}) %collective-permute-start.13) | collective-permute-done | bytes 57376 | tf_op jit(solution)/shard_map/ppermute | solution.py:227
  97.8 2.6 %collective-permute-start.14 = (bf16[56,512]{1,0:T(8,128)(2,1)S(1)}, bf16[56,512]{1,0:T(8,128)(2,1)S(1)}, u32[]{:S(2)}, u32[]{:S(2)}) collective-permute-start(bf16[56,512]{1,0:T(8,128)(2,1)S(1)} %add_convert_fusion.12), channel_id=1, source_target_pairs={{0,4},{4,0},{8,12},{12,8},{16,20},{20,16},{24,28},{28,24},{1,5},{5... | collective-permute-start | bytes 172040 | tf_op jit(solution)/shard_map/ppermute | solution.py:227
  102.6 4.2 %collective-permute-start.10 = (bf16[3,6,512]{2,1,0:T(8,128)(2,1)S(1)}, bf16[3,6,512]{2,1,0:T(8,128)(2,1)S(1)}, u32[]{:S(2)}, u32[]{:S(2)}) collective-permute-start(bf16[3,6,512]{2,1,0:T(8,128)(2,1)S(1)} %get-tuple-element.57), channel_id=1, source_target_pairs={{0,4},{4,8},{8,12},{12,16},{16,20},{20,24},{24,28},{1,5},{5,9},{9,... | collective-permute-start | bytes 55304 | tf_op jit(solution)/shard_map/ppermute | solution.py:205
  110.4 12.0 %collective-permute-done.28 = bf16[128,2048]{1,0:T(8,128)(2,1)S(1)} collective-permute-done((bf16[128,2048]{1,0:T(8,128)(2,1)S(1)}, bf16[128,2048]{1,0:T(8,128)(2,1)S(1)}, u32[]{:S(2)}, u32[]{:S(2)}) %collective-permute-start.28) | collective-permute-done | bytes 524320 | tf_op jit(solution)/shard_map/ppermute | solution.py:227
  123.6 11.4 %collective-permute-done.18 = bf16[128,2048]{1,0:T(8,128)(2,1)S(1)} collective-permute-done((bf16[128,2048]{1,0:T(8,128)(2,1)S(1)}, bf16[128,2048]{1,0:T(8,128)(2,1)S(1)}, u32[]{:S(2)}, u32[]{:S(2)}) %collective-permute-start.18) | collective-permute-done | bytes 524320 | tf_op jit(solution)/shard_map/ppermute | solution.py:227
  136.5 4.9 %collective-permute-done.29 = bf16[64,2048]{1,0:T(8,128)(2,1)S(1)} collective-permute-done((bf16[64,2048]{1,0:T(8,128)(2,1)S(1)}, bf16[64,2048]{1,0:T(8,128)(2,1)S(1)}, u32[]{:S(2)}, u32[]{:S(2)}) %collective-permute-start.29) | collective-permute-done | bytes 262176 | tf_op jit(solution)/shard_map/ppermute | solution.py:227
  142.0 7.2 %collective-permute-done.19 = bf16[64,2048]{1,0:T(8,128)(2,1)S(1)} collective-permute-done((bf16[64,2048]{1,0:T(8,128)(2,1)S(1)}, bf16[64,2048]{1,0:T(8,128)(2,1)S(1)}, u32[]{:S(2)}, u32[]{:S(2)}) %collective-permute-start.19) | collective-permute-done | bytes 262176 | tf_op jit(solution)/shard_map/ppermute | solution.py:227
  149.7 5.8 %collective-permute-done.30 = bf16[32,2048]{1,0:T(8,128)(2,1)S(1)} collective-permute-done((bf16[32,2048]{1,0:T(8,128)(2,1)S(1)}, bf16[32,2048]{1,0:T(8,128)(2,1)S(1)}, u32[]{:S(2)}, u32[]{:S(2)}) %collective-permute-start.30) | collective-permute-done | bytes 131104 | tf_op jit(solution)/shard_map/ppermute | solution.py:227
  155.9 6.8 %collective-permute-done.20 = bf16[32,2048]{1,0:T(8,128)(2,1)S(1)} collective-permute-done((bf16[32,2048]{1,0:T(8,128)(2,1)S(1)}, bf16[32,2048]{1,0:T(8,128)(2,1)S(1)}, u32[]{:S(2)}, u32[]{:S(2)}) %collective-permute-start.20) | collective-permute-done | bytes 131104 | tf_op jit(solution)/shard_map/ppermute | solution.py:227
  162.7 6.3 %collective-permute-done.31 = bf16[16,2048]{1,0:T(8,128)(2,1)S(1)} collective-permute-done((bf16[16,2048]{1,0:T(8,128)(2,1)S(1)}, bf16[16,2048]{1,0:T(8,128)(2,1)S(1)}, u32[]{:S(2)}, u32[]{:S(2)}) %collective-permute-start.31) | collective-permute-done | bytes 65568 | tf_op jit(solution)/shard_map/ppermute | solution.py:227
  169.0 4.2 %collective-permute-done.21 = bf16[16,2048]{1,0:T(8,128)(2,1)S(1)} collective-permute-done((bf16[16,2048]{1,0:T(8,128)(2,1)S(1)}, bf16[16,2048]{1,0:T(8,128)(2,1)S(1)}, u32[]{:S(2)}, u32[]{:S(2)}) %collective-permute-start.21) | collective-permute-done | bytes 65568 | tf_op jit(solution)/shard_map/ppermute | solution.py:227
  173.3 5.1 %collective-permute-done.32 = bf16[16,2048]{1,0:T(8,128)(2,1)S(1)} collective-permute-done((bf16[16,2048]{1,0:T(8,128)(2,1)S(1)}, bf16[16,2048]{1,0:T(8,128)(2,1)S(1)}, u32[]{:S(2)}, u32[]{:S(2)}) %collective-permute-start.32) | collective-permute-done | bytes 65568 | tf_op jit(solution)/shard_map/ppermute | solution.py:227
  178.8 3.9 %collective-permute-done.22 = bf16[16,2048]{1,0:T(8,128)(2,1)S(1)} collective-permute-done((bf16[16,2048]{1,0:T(8,128)(2,1)S(1)}, bf16[16,2048]{1,0:T(8,128)(2,1)S(1)}, u32[]{:S(2)}, u32[]{:S(2)}) %collective-permute-start.22) | collective-permute-done | bytes 65568 | tf_op jit(solution)/shard_map/ppermute | solution.py:227
  182.7 4.9 %collective-permute-done.33 = bf16[32,2048]{1,0:T(8,128)(2,1)S(1)} collective-permute-done((bf16[32,2048]{1,0:T(8,128)(2,1)S(1)}, bf16[32,2048]{1,0:T(8,128)(2,1)S(1)}, u32[]{:S(2)}, u32[]{:S(2)}) %collective-permute-start.33) | collective-permute-done | bytes 131104 | tf_op jit(solution)/shard_map/ppermute | solution.py:227
  188.2 6.5 %collective-permute-done.23 = bf16[32,2048]{1,0:T(8,128)(2,1)S(1)} collective-permute-done((bf16[32,2048]{1,0:T(8,128)(2,1)S(1)}, bf16[32,2048]{1,0:T(8,128)(2,1)S(1)}, u32[]{:S(2)}, u32[]{:S(2)}) %collective-permute-start.23) | collective-permute-done | bytes 131104 | tf_op jit(solution)/shard_map/ppermute | solution.py:227
  196.0 5.0 %collective-permute-done.34 = bf16[64,2048]{1,0:T(8,128)(2,1)S(1)} collective-permute-done((bf16[64,2048]{1,0:T(8,128)(2,1)S(1)}, bf16[64,2048]{1,0:T(8,128)(2,1)S(1)}, u32[]{:S(2)}, u32[]{:S(2)}) %collective-permute-start.34) | collective-permute-done | bytes 262176 | tf_op jit(solution)/shard_map/ppermute | solution.py:227
  201.5 5.9 %collective-permute-done.24 = bf16[64,2048]{1,0:T(8,128)(2,1)S(1)} collective-permute-done((bf16[64,2048]{1,0:T(8,128)(2,1)S(1)}, bf16[64,2048]{1,0:T(8,128)(2,1)S(1)}, u32[]{:S(2)}, u32[]{:S(2)}) %collective-permute-start.24) | collective-permute-done | bytes 262176 | tf_op jit(solution)/shard_map/ppermute | solution.py:227
  207.9 8.7 %collective-permute-done.35 = bf16[128,2048]{1,0:T(8,128)(2,1)S(1)} collective-permute-done((bf16[128,2048]{1,0:T(8,128)(2,1)S(1)}, bf16[128,2048]{1,0:T(8,128)(2,1)S(1)}, u32[]{:S(2)}, u32[]{:S(2)}) %collective-permute-start.35) | collective-permute-done | bytes 524320 | tf_op jit(solution)/shard_map/ppermute | solution.py:227
  218.4 7.5 %collective-permute-done.25 = bf16[128,2048]{1,0:T(8,128)(2,1)S(1)} collective-permute-done((bf16[128,2048]{1,0:T(8,128)(2,1)S(1)}, bf16[128,2048]{1,0:T(8,128)(2,1)S(1)}, u32[]{:S(2)}, u32[]{:S(2)}) %collective-permute-start.25) | collective-permute-done | bytes 524320 | tf_op jit(solution)/shard_map/ppermute | solution.py:227
  233.5 12.5 %spread.1 = bf16[8,128,512]{2,1,0:T(8,128)(2,1)} custom-call(bf16[8,128,512]{2,1,0:T(8,128)(2,1)S(1)} %bitcast.17, bf16[3,128,512]{2,1,0:T(8,128)(2,1)S(1)} %collective-permute-done.6.top, bf16[3,128,512]{2,1,0:T(8,128)(2,1)S(1)} %collective-permute-done.7.bot, bf16[8,3,512]{2,1,0:T(4,128)(2,1)S(1)} %collective-permute-done.8.lft, ...), custom_call_target="tpu_custom_call" | custom-call | tf_op jit(solution)/shard_map/spread/pallas_call | solution.py:195
  249.2 5.3 %copy.13 = f32[2048,512]{1,0:T(8,128)} copy(f32[2048,512]{0,1:T(8,128)} %convert_bitcast_fusion) | data formatting | bytes 8388608
  254.9 2.6 maximum_convert_fusion
  (128 shorter events, 46.4 us)
Async XLA Ops:
  2.9 25.1 %collective-permute-start = (bf16[3,128,512]{2,1,0:T(8,128)(2,1)}, bf16[3,128,512]{2,1,0:T(8,128)(2,1)S(1)}, u32[]{:S(2)}, u32[]{:S(2)}) collective-permute-start(bf16[3,128,512]{2,1,0:T(8,128)(2,1)} %get-tuple-element.43), channel_id=1, source_target_pairs={{0,4},{4,8},{8,12},{12,16},{16,20},{20,24},{24,28},{1,5},{5,9},{9,... | collective-permute-start | bytes 1179656 | tf_op jit(solution)/shard_map/ppermute | solution.py:205
  7.8 20.2 %collective-permute-start.1 = (bf16[3,128,512]{2,1,0:T(8,128)(2,1)}, bf16[3,128,512]{2,1,0:T(8,128)(2,1)}, u32[]{:S(2)}, u32[]{:S(2)}) collective-permute-start(bf16[3,128,512]{2,1,0:T(8,128)(2,1)} %get-tuple-element.42), channel_id=1, source_target_pairs={{4,0},{8,4},{12,8},{16,12},{20,16},{24,20},{28,24},{5,1},{9,5},{13... | collective-permute-start | bytes 1179656 | tf_op jit(solution)/shard_map/ppermute | solution.py:205
  11.5 4.7 %collective-permute-start.3 = (bf16[8,3,512]{2,1,0:T(4,128)(2,1)S(1)}, bf16[8,3,512]{2,1,0:T(4,128)(2,1)S(1)}, u32[]{:S(2)}, u32[]{:S(2)}) collective-permute-start(bf16[8,3,512]{2,1,0:T(4,128)(2,1)S(1)} %get-tuple-element.40), channel_id=1, source_target_pairs={{1,0},{2,1},{3,2},{5,4},{6,5},{7,6},{9,8},{10,9},{11,10},{13,12},{... | collective-permute-start | bytes 73736 | tf_op jit(solution)/shard_map/ppermute | solution.py:205
  16.8 8.5 %collective-permute-start.4 = (bf16[3,6,512]{2,1,0:T(8,128)(2,1)}, bf16[3,6,512]{2,1,0:T(8,128)(2,1)}, u32[]{:S(2)}, u32[]{:S(2)}) collective-permute-start(bf16[3,6,512]{2,1,0:T(8,128)(2,1)} %get-tuple-element.59), channel_id=1, source_target_pairs={{0,4},{4,8},{8,12},{12,16},{16,20},{20,24},{24,28},{1,5},{5,9},{9,... | collective-permute-start | bytes 55304 | tf_op jit(solution)/shard_map/ppermute | solution.py:205
  21.9 6.0 %collective-permute-start.5 = (bf16[3,6,512]{2,1,0:T(8,128)(2,1)}, bf16[3,6,512]{2,1,0:T(8,128)(2,1)}, u32[]{:S(2)}, u32[]{:S(2)}) collective-permute-start(bf16[3,6,512]{2,1,0:T(8,128)(2,1)} %get-tuple-element.58), channel_id=1, source_target_pairs={{4,0},{8,4},{12,8},{16,12},{20,16},{24,20},{28,24},{5,1},{9,5},{13... | collective-permute-start | bytes 55304 | tf_op jit(solution)/shard_map/ppermute | solution.py:205
  69.4 164.1 %collective-permute-start.6 = (bf16[3,128,512]{2,1,0:T(8,128)(2,1)S(1)}, bf16[3,128,512]{2,1,0:T(8,128)(2,1)S(1)}, u32[]{:S(2)}, u32[]{:S(2)}) collective-permute-start(bf16[3,128,512]{2,1,0:T(8,128)(2,1)S(1)} %bitcast.25), channel_id=1, source_target_pairs={{0,4},{4,8},{8,12},{12,16},{16,20},{20,24},{24,28},{1,5},{5,9},{9,... | collective-permute-start | bytes 1179656 | tf_op jit(solution)/shard_map/ppermute | solution.py:205
  74.2 159.4 %collective-permute-start.7 = (bf16[3,128,512]{2,1,0:T(8,128)(2,1)S(1)}, bf16[3,128,512]{2,1,0:T(8,128)(2,1)S(1)}, u32[]{:S(2)}, u32[]{:S(2)}) collective-permute-start(bf16[3,128,512]{2,1,0:T(8,128)(2,1)S(1)} %bitcast.24), channel_id=1, source_target_pairs={{4,0},{8,4},{12,8},{16,12},{20,16},{24,20},{28,24},{5,1},{9,5},{13... | collective-permute-start | bytes 1179656 | tf_op jit(solution)/shard_map/ppermute | solution.py:205
  75.5 20.5 %collective-permute-start.8 = (bf16[8,3,512]{2,1,0:T(4,128)(2,1)S(1)}, bf16[8,3,512]{2,1,0:T(4,128)(2,1)S(1)}, u32[]{:S(2)}, u32[]{:S(2)}) collective-permute-start(bf16[8,3,512]{2,1,0:T(4,128)(2,1)S(1)} %get-tuple-element.37), channel_id=1, source_target_pairs={{0,1},{1,2},{2,3},{4,5},{5,6},{6,7},{8,9},{9,10},{10,11},{12,13},{... | collective-permute-start | bytes 73736 | tf_op jit(solution)/shard_map/ppermute | solution.py:205
  89.7 17.1 %collective-permute-start.27 = (bf16[256,2048]{1,0:T(8,128)(2,1)S(1)}, bf16[256,2048]{1,0:T(8,128)(2,1)S(1)}, u32[]{:S(2)}, u32[]{:S(2)}) collective-permute-start(bf16[256,2048]{1,0:T(8,128)(2,1)S(1)} %constant_dynamic-slice_fusion.4), channel_id=1, source_target_pairs={{0,1},{1,0},{2,3},{3,2},{4,5},{5,4},{6,7},{7,6},{8,9},{9,8},{10,11... | collective-permute-start | bytes 3145736 | tf_op jit(solution)/shard_map/ppermute | solution.py:227
  96.0 12.8 %collective-permute-start.17 = (bf16[256,2048]{1,0:T(8,128)(2,1)S(1)}, bf16[256,2048]{1,0:T(8,128)(2,1)S(1)}, u32[]{:S(2)}, u32[]{:S(2)}) collective-permute-start(bf16[256,2048]{1,0:T(8,128)(2,1)S(1)} %constant_dynamic-slice_fusion.9), channel_id=1, source_target_pairs={{0,1},{1,0},{2,3},{3,2},{4,5},{5,4},{6,7},{7,6},{8,9},{9,8},{10,11... | collective-permute-start | bytes 3145736 | tf_op jit(solution)/shard_map/ppermute | solution.py:227
  97.8 4.8 %collective-permute-start.14 = (bf16[56,512]{1,0:T(8,128)(2,1)S(1)}, bf16[56,512]{1,0:T(8,128)(2,1)S(1)}, u32[]{:S(2)}, u32[]{:S(2)}) collective-permute-start(bf16[56,512]{1,0:T(8,128)(2,1)S(1)} %add_convert_fusion.12), channel_id=1, source_target_pairs={{0,4},{4,0},{8,12},{12,8},{16,20},{20,16},{24,28},{28,24},{1,5},{5... | collective-permute-start | bytes 172040 | tf_op jit(solution)/shard_map/ppermute | solution.py:227
  102.6 125.2 %collective-permute-start.10 = (bf16[3,6,512]{2,1,0:T(8,128)(2,1)S(1)}, bf16[3,6,512]{2,1,0:T(8,128)(2,1)S(1)}, u32[]{:S(2)}, u32[]{:S(2)}) collective-permute-start(bf16[3,6,512]{2,1,0:T(8,128)(2,1)S(1)} %get-tuple-element.57), channel_id=1, source_target_pairs={{0,4},{4,8},{8,12},{12,16},{16,20},{20,24},{24,28},{1,5},{5,9},{9,... | collective-permute-start | bytes 55304 | tf_op jit(solution)/shard_map/ppermute | solution.py:205
  106.8 111.4 %collective-permute-start.15 = (bf16[56,512]{1,0:T(8,128)(2,1)S(1)}, bf16[56,512]{1,0:T(8,128)(2,1)S(1)}, u32[]{:S(2)}, u32[]{:S(2)}) collective-permute-start(bf16[56,512]{1,0:T(8,128)(2,1)S(1)} %add_convert_fusion.11), channel_id=1, source_target_pairs={{0,8},{4,12},{8,0},{12,4},{16,24},{20,28},{24,16},{28,20},{1,9},{5... | collective-permute-start | bytes 172040 | tf_op jit(solution)/shard_map/ppermute | solution.py:227
  108.9 13.5 %collective-permute-start.28 = (bf16[128,2048]{1,0:T(8,128)(2,1)S(1)}, bf16[128,2048]{1,0:T(8,128)(2,1)S(1)}, u32[]{:S(2)}, u32[]{:S(2)}) collective-permute-start(bf16[128,2048]{1,0:T(8,128)(2,1)S(1)} %constant_dynamic-slice_fusion.3), channel_id=1, source_target_pairs={{0,2},{1,3},{2,0},{3,1},{4,6},{5,7},{6,4},{7,5},{8,10},{9,11},{10,... | collective-permute-start | bytes 1572872 | tf_op jit(solution)/shard_map/ppermute | solution.py:227
  122.4 12.6 %collective-permute-start.18 = (bf16[128,2048]{1,0:T(8,128)(2,1)S(1)}, bf16[128,2048]{1,0:T(8,128)(2,1)S(1)}, u32[]{:S(2)}, u32[]{:S(2)}) collective-permute-start(bf16[128,2048]{1,0:T(8,128)(2,1)S(1)} %constant_dynamic-slice_fusion.8), channel_id=1, source_target_pairs={{0,4},{4,0},{8,12},{12,8},{16,20},{20,16},{24,28},{28,24},{1,5},{5... | collective-permute-start | bytes 1572872 | tf_op jit(solution)/shard_map/ppermute | solution.py:227
  135.0 6.4 %collective-permute-start.29 = (bf16[64,2048]{1,0:T(8,128)(2,1)S(1)}, bf16[64,2048]{1,0:T(8,128)(2,1)S(1)}, u32[]{:S(2)}, u32[]{:S(2)}) collective-permute-start(bf16[64,2048]{1,0:T(8,128)(2,1)S(1)} %constant_dynamic-slice_fusion.2), channel_id=1, source_target_pairs={{0,4},{4,0},{8,12},{12,8},{16,20},{20,16},{24,28},{28,24},{1,5},{5... | collective-permute-start | bytes 786440 | tf_op jit(solution)/shard_map/ppermute | solution.py:227
  141.4 7.8 %collective-permute-start.19 = (bf16[64,2048]{1,0:T(8,128)(2,1)S(1)}, bf16[64,2048]{1,0:T(8,128)(2,1)S(1)}, u32[]{:S(2)}, u32[]{:S(2)}) collective-permute-start(bf16[64,2048]{1,0:T(8,128)(2,1)S(1)} %constant_dynamic-slice_fusion.7), channel_id=1, source_target_pairs={{0,8},{4,12},{8,0},{12,4},{16,24},{20,28},{24,16},{28,20},{1,9},{5... | collective-permute-start | bytes 786440 | tf_op jit(solution)/shard_map/ppermute | solution.py:227
  149.2 6.3 %collective-permute-start.30 = (bf16[32,2048]{1,0:T(8,128)(2,1)S(1)}, bf16[32,2048]{1,0:T(8,128)(2,1)S(1)}, u32[]{:S(2)}, u32[]{:S(2)}) collective-permute-start(bf16[32,2048]{1,0:T(8,128)(2,1)S(1)} %constant_dynamic-slice_fusion.1), channel_id=1, source_target_pairs={{0,8},{4,12},{8,0},{12,4},{16,24},{20,28},{24,16},{28,20},{1,9},{5... | collective-permute-start | bytes 393224 | tf_op jit(solution)/shard_map/ppermute | solution.py:227
  155.5 7.1 %collective-permute-start.20 = (bf16[32,2048]{1,0:T(8,128)(2,1)S(1)}, bf16[32,2048]{1,0:T(8,128)(2,1)S(1)}, u32[]{:S(2)}, u32[]{:S(2)}) collective-permute-start(bf16[32,2048]{1,0:T(8,128)(2,1)S(1)} %constant_dynamic-slice_fusion.6), channel_id=1, source_target_pairs={{0,16},{4,20},{8,24},{12,28},{16,0},{20,4},{24,8},{28,12},{1,17},{... | collective-permute-start | bytes 393224 | tf_op jit(solution)/shard_map/ppermute | solution.py:227
  162.6 6.4 %collective-permute-start.31 = (bf16[16,2048]{1,0:T(8,128)(2,1)S(1)}, bf16[16,2048]{1,0:T(8,128)(2,1)S(1)}, u32[]{:S(2)}, u32[]{:S(2)}) collective-permute-start(bf16[16,2048]{1,0:T(8,128)(2,1)S(1)} %constant_dynamic-slice_fusion), channel_id=1, source_target_pairs={{0,16},{4,20},{8,24},{12,28},{16,0},{20,4},{24,8},{28,12},{1,17},{... | collective-permute-start | bytes 196616 | tf_op jit(solution)/shard_map/ppermute | solution.py:227
  169.0 4.3 %collective-permute-start.21 = (bf16[16,2048]{1,0:T(8,128)(2,1)S(1)}, bf16[16,2048]{1,0:T(8,128)(2,1)S(1)}, u32[]{:S(2)}, u32[]{:S(2)}) collective-permute-start(bf16[16,2048]{1,0:T(8,128)(2,1)S(1)} %constant_dynamic-slice_fusion.5), channel_id=1, source_target_pairs={{0,2},{1,3},{2,0},{3,1},{4,6},{5,7},{6,4},{7,5},{8,10},{9,11},{10,... | collective-permute-start | bytes 196616 | tf_op jit(solution)/shard_map/ppermute | solution.py:227
  173.3 5.2 %collective-permute-start.32 = (bf16[16,2048]{1,0:T(8,128)(2,1)S(1)}, bf16[16,2048]{1,0:T(8,128)(2,1)S(1)}, u32[]{:S(2)}, u32[]{:S(2)}) collective-permute-start(bf16[16,2048]{1,0:T(8,128)(2,1)S(1)} %add_convert_fusion.8), channel_id=1, source_target_pairs={{0,16},{4,20},{8,24},{12,28},{16,0},{20,4},{24,8},{28,12},{1,17},{... | collective-permute-start | bytes 196616 | tf_op jit(solution)/shard_map/ppermute | solution.py:227
  182.7 5.0 %collective-permute-start.33 = (bf16[32,2048]{1,0:T(8,128)(2,1)S(1)}, bf16[32,2048]{1,0:T(8,128)(2,1)S(1)}, u32[]{:S(2)}, u32[]{:S(2)}) collective-permute-start(bf16[32,2048]{1,0:T(8,128)(2,1)S(1)} %pad_maximum_fusion.7), channel_id=1, source_target_pairs={{0,8},{4,12},{8,0},{12,4},{16,24},{20,28},{24,16},{28,20},{1,9},{5... | collective-permute-start | bytes 393224 | tf_op jit(solution)/shard_map/ppermute | solution.py:227
  187.7 7.0 %collective-permute-start.23 = (bf16[32,2048]{1,0:T(8,128)(2,1)S(1)}, bf16[32,2048]{1,0:T(8,128)(2,1)S(1)}, u32[]{:S(2)}, u32[]{:S(2)}) collective-permute-start(bf16[32,2048]{1,0:T(8,128)(2,1)S(1)} %pad_maximum_fusion.6), channel_id=1, source_target_pairs={{0,16},{4,20},{8,24},{12,28},{16,0},{20,4},{24,8},{28,12},{1,17},{... | collective-permute-start | bytes 393224 | tf_op jit(solution)/shard_map/ppermute | solution.py:227
  194.7 6.4 %collective-permute-start.34 = (bf16[64,2048]{1,0:T(8,128)(2,1)S(1)}, bf16[64,2048]{1,0:T(8,128)(2,1)S(1)}, u32[]{:S(2)}, u32[]{:S(2)}) collective-permute-start(bf16[64,2048]{1,0:T(8,128)(2,1)S(1)} %pad_maximum_fusion.5), channel_id=1, source_target_pairs={{0,4},{4,0},{8,12},{12,8},{16,20},{20,16},{24,28},{28,24},{1,5},{5... | collective-permute-start | bytes 786440 | tf_op jit(solution)/shard_map/ppermute | solution.py:227
  201.0 6.4 %collective-permute-start.24 = (bf16[64,2048]{1,0:T(8,128)(2,1)S(1)}, bf16[64,2048]{1,0:T(8,128)(2,1)S(1)}, u32[]{:S(2)}, u32[]{:S(2)}) collective-permute-start(bf16[64,2048]{1,0:T(8,128)(2,1)S(1)} %pad_maximum_fusion.4), channel_id=1, source_target_pairs={{0,8},{4,12},{8,0},{12,4},{16,24},{20,28},{24,16},{28,20},{1,9},{5... | collective-permute-start | bytes 786440 | tf_op jit(solution)/shard_map/ppermute | solution.py:227
  207.4 9.2 %collective-permute-start.35 = (bf16[128,2048]{1,0:T(8,128)(2,1)S(1)}, bf16[128,2048]{1,0:T(8,128)(2,1)S(1)}, u32[]{:S(2)}, u32[]{:S(2)}) collective-permute-start(bf16[128,2048]{1,0:T(8,128)(2,1)S(1)} %pad_maximum_fusion.3), channel_id=1, source_target_pairs={{0,2},{1,3},{2,0},{3,1},{4,6},{5,7},{6,4},{7,5},{8,10},{9,11},{10,... | collective-permute-start | bytes 1572872 | tf_op jit(solution)/shard_map/ppermute | solution.py:227
  216.6 9.3 %collective-permute-start.25 = (bf16[128,2048]{1,0:T(8,128)(2,1)S(1)}, bf16[128,2048]{1,0:T(8,128)(2,1)S(1)}, u32[]{:S(2)}, u32[]{:S(2)}) collective-permute-start(bf16[128,2048]{1,0:T(8,128)(2,1)S(1)} %pad_maximum_fusion.2), channel_id=1, source_target_pairs={{0,4},{4,0},{8,12},{12,8},{16,20},{20,16},{24,28},{28,24},{1,5},{5... | collective-permute-start | bytes 1572872 | tf_op jit(solution)/shard_map/ppermute | solution.py:227
  218.3 27.8 %collective-permute-start.36 = (bf16[256,2048]{1,0:T(8,128)(2,1)S(1)}, bf16[256,2048]{1,0:T(8,128)(2,1)S(1)}, u32[]{:S(2)}, u32[]{:S(2)}) collective-permute-start(bf16[256,2048]{1,0:T(8,128)(2,1)S(1)} %pad_maximum_fusion.1), channel_id=1, source_target_pairs={{0,1},{1,0},{2,3},{3,2},{4,5},{5,4},{6,7},{7,6},{8,9},{9,8},{10,11... | collective-permute-start | bytes 3145736 | tf_op jit(solution)/shard_map/ppermute | solution.py:227
  225.9 5.3 %collective-permute-start.16 = (bf16[56,512]{1,0:T(8,128)(2,1)S(1)}, bf16[56,512]{1,0:T(8,128)(2,1)S(1)}, u32[]{:S(2)}, u32[]{:S(2)}) collective-permute-start(bf16[56,512]{1,0:T(8,128)(2,1)S(1)} %add_convert_fusion.10), channel_id=1, source_target_pairs={{0,16},{4,20},{8,24},{12,28},{16,0},{20,4},{24,8},{28,12},{1,17},{... | collective-permute-start | bytes 172040 | tf_op jit(solution)/shard_map/ppermute | solution.py:227
  227.8 5.7 %collective-permute-start.11 = (bf16[3,6,512]{2,1,0:T(8,128)(2,1)S(1)}, bf16[3,6,512]{2,1,0:T(8,128)(2,1)S(1)}, u32[]{:S(2)}, u32[]{:S(2)}) collective-permute-start(bf16[3,6,512]{2,1,0:T(8,128)(2,1)S(1)} %get-tuple-element.56), channel_id=1, source_target_pairs={{4,0},{8,4},{12,8},{16,12},{20,16},{24,20},{28,24},{5,1},{9,5},{13... | collective-permute-start | bytes 55304 | tf_op jit(solution)/shard_map/ppermute | solution.py:205
  231.2 23.3 %collective-permute-start.26 = (bf16[256,2048]{1,0:T(8,128)(2,1)}, bf16[256,2048]{1,0:T(8,128)(2,1)S(1)}, u32[]{:S(2)}, u32[]{:S(2)}) collective-permute-start(bf16[256,2048]{1,0:T(8,128)(2,1)} %pad_maximum_fusion), channel_id=1, source_target_pairs={{0,1},{1,0},{2,3},{3,2},{4,5},{5,4},{6,7},{7,6},{8,9},{9,8},{10,11... | collective-permute-start | bytes 3145736 | tf_op jit(solution)/shard_map/ppermute | solution.py:227
  (18 other events, 197.7 us)
